TPU v7x, 32 devices: a whole 2x2x4 slice. The times are simulated.
32 devices in a mesh: owner: 8 (over z, y), rep: 4 (over x, core).
Axes of the slice: x: 2, y: 2, z: 4, core: 2. Of those that a mesh axis runs over, the one named last changes fastest.
Arguments:
- bin_blocks: int32 [8192], P(('owner', 'rep')), may hold values from 0 to 2047, as said below
- send_counts: int32 [32, 8], P(('owner', 'rep')), may hold values from 0 to 64, as said below
- voxel_index: int32 [8192, 128], P(('owner', 'rep')), may hold values from 0 to 511
- point_sdf: bfloat16 [8192, 128], P(('owner', 'rep')), may hold values from -1 to 1
- point_weight: bfloat16 [8192, 128], P(('owner', 'rep')), may hold values from 0.099609375 to 1
- point_color: bfloat16 [8192, 3, 128], P(('owner', 'rep')), may hold values from 0 to 1
- owner_table: int32 [2048], replicated, may hold values from 0 to 2047, as said below
- old_tsdf: float32 [2048, 4, 512], P(('owner', 'rep')), may hold values from -1 to 1
- old_weight: float32 [2048, 512], P(('owner', 'rep')), may hold values from 0.5 to 4
Outputs:
- new_tsdf: float32 [2048, 4, 512], P(('owner', 'rep'))
- new_weight: float32 [2048, 512], P(('owner', 'rep'))
Inputs may be any that keep to these rules, and one draw needn't show every extreme that they name: `send_counts`: each row sums to 256; every row has an entry equal to 64; among the devices s with the same s mod 4 (one frame group), some owner receives 64 bins from every one of them. `owner_table`: a permutation; entry g is the owner of block g times 256 plus the block's place among that owner's blocks. `bin_blocks`: owner_table assigns the block of bin j of device s to owner p(s, j) of the first step; of the bins that one frame group sends to one owner, at most 128 have places in any one quarter of its 256 places (places q * 64 to (q + 1) * 64 - 1), and this most is reached in every frame group.
All inputs are finite; a program needn't handle non-finite values.
Results may differ from a plain program's by a relative error of at most 0.00078.
Values may be sent and summed in bfloat16 or wider, within the bound.
A program may use at most 64 MiB of HBM per device.

v0:
```python
import math

import jax
import jax.numpy as jnp
from jax import lax
from jax.experimental import pallas as pl
from jax.experimental.pallas import tpu as pltpu
from jax.sharding import PartitionSpec as P

OWN = 256
VA = 8
VB = 64


def accumulate(feature_list, voxels, block_rows, block_total):
    slot_count, points = voxels.shape
    group_size = math.gcd(slot_count, 128)
    group_count = slot_count // group_size
    channels = sum_channels(feature_list)
    grouped = tuple((f.reshape((group_count, group_size) + f.shape[1:]) for f in feature_list))
    voxel_groups = voxels.reshape(group_count, group_size, points)
    block_groups = jnp.maximum(block_rows, 0).reshape(group_count, group_size)
    upper_ids = jnp.arange(VA, dtype=jnp.int32)
    lower_ids = jnp.arange(VB, dtype=jnp.int32)

    def fold_group(running, pieces):
        feature_parts, voxel_rows, block_ids = pieces
        features_group = jnp.concatenate(list(feature_parts), axis=1)
        upper_part = voxel_rows // VB
        lower_part = voxel_rows % VB
        chosen = upper_part[:, None, :] == upper_ids[None, :, None]
        left_side = jnp.where(
            chosen[:, None], features_group[:, :, None, :], jnp.zeros((), jnp.bfloat16)
        )
        left_side = left_side.reshape(group_size, channels * VA, points)
        right_side = (lower_part[:, :, None] == lower_ids[None, None, :]).astype(jnp.bfloat16)
        slot_grids = jnp.einsum(
            "gkp,gpb->gkb", left_side, right_side, preferred_element_type=jnp.float32
        )
        slot_grids = slot_grids.reshape(group_size, channels, VA * VB)
        return (running.at[block_ids].add(slot_grids), None)

    running_start = jnp.zeros((block_total, channels, VA * VB), jnp.float32)
    running_end, _ = lax.scan(fold_group, running_start, (grouped, voxel_groups, block_groups))
    return running_end


def sum_channels(feature_list):
    total_channels = 0
    for member in feature_list:
        total_channels = total_channels + member.shape[1]
    return total_channels


def local(
    bin_blocks,
    send_counts,
    voxel_index,
    point_sdf,
    point_weight,
    point_color,
    owner_table,
    old_tsdf,
    old_weight,
):
    owners = lax.axis_size("owner")
    bin_count = bin_blocks.shape[0]
    capacity = 2 * bin_count // owners
    slot_count = owners * capacity
    counts = send_counts[0]
    starts = jnp.cumsum(counts) - counts
    slot_ids = jnp.arange(slot_count, dtype=jnp.int32)
    target = slot_ids // capacity
    position = slot_ids % capacity
    active = position < counts[target]
    source = jnp.clip(starts[target] + position, 0, bin_count - 1)
    blocks_sent = jnp.where(active, owner_table[bin_blocks[source]] % OWN, -1)
    weight = jnp.where(active[:, None], point_weight[source], jnp.zeros((), jnp.bfloat16))
    wide_weight = weight.astype(jnp.float32)
    weighted_sdf = (wide_weight * point_sdf[source].astype(jnp.float32)).astype(jnp.bfloat16)
    geometry = jnp.stack([weight, weighted_sdf], axis=1)
    colors = (wide_weight[:, None, :] * point_color[source].astype(jnp.float32)).astype(
        jnp.bfloat16
    )
    voxels = voxel_index[source]
    replicas = lax.axis_size("rep")
    share = OWN // replicas
    arrived_geometry, arrived_colors, arrived_voxels, arrived_blocks = (
        lax.all_to_all(geometry, "owner", split_axis=0, concat_axis=0, tiled=True),
        lax.all_to_all(colors, "owner", split_axis=0, concat_axis=0, tiled=True),
        lax.all_to_all(voxels, "owner", split_axis=0, concat_axis=0, tiled=True),
        lax.all_to_all(blocks_sent, "owner", split_axis=0, concat_axis=0, tiled=True),
    )
    quota = 2 * bin_count // replicas
    live = arrived_blocks >= 0
    quarter = jnp.where(live, arrived_blocks // share, 0)
    quarter_ids = jnp.arange(replicas, dtype=jnp.int32)
    member = (live[:, None] & (quarter[:, None] == quarter_ids[None, :])).astype(jnp.int32)
    rank = jnp.sum((jnp.cumsum(member, axis=0) - member) * member, axis=1)
    outgoing_slots = replicas * quota
    destination = jnp.where(live, quarter * quota + rank, outgoing_slots).astype(jnp.int32)
    arrived_ids = jnp.arange(arrived_blocks.shape[0], dtype=jnp.int32)
    picked = jnp.zeros((outgoing_slots,), jnp.int32).at[destination].set(arrived_ids, mode="drop")
    filled = jnp.zeros((outgoing_slots,), jnp.bool_).at[destination].set(True, mode="drop")
    send_geometry = jnp.where(
        filled[:, None, None], arrived_geometry[picked], jnp.zeros((), jnp.bfloat16)
    )
    send_colors = jnp.where(
        filled[:, None, None], arrived_colors[picked], jnp.zeros((), jnp.bfloat16)
    )
    send_voxels = arrived_voxels[picked]
    send_places = jnp.where(filled, arrived_blocks[picked] % share, -1).astype(jnp.int32)
    final_geometry, final_colors, final_voxels, final_places = (
        lax.all_to_all(send_geometry, "rep", split_axis=0, concat_axis=0, tiled=True),
        lax.all_to_all(send_colors, "rep", split_axis=0, concat_axis=0, tiled=True),
        lax.all_to_all(send_voxels, "rep", split_axis=0, concat_axis=0, tiled=True),
        lax.all_to_all(send_places, "rep", split_axis=0, concat_axis=0, tiled=True),
    )
    cell_sums = accumulate((final_geometry, final_colors), final_voxels, final_places, share)
    geometry_share = cell_sums[:, :2]
    color_share = cell_sums[:, 2:]
    new_weight = old_weight + geometry_share[:, 0]
    joined_sdf = (old_weight * old_tsdf[:, 0] + geometry_share[:, 1]) / new_weight
    joined_color = (old_weight[:, None, :] * old_tsdf[:, 1:] + color_share) / new_weight[:, None, :]
    new_tsdf = jnp.concatenate([joined_sdf[:, None, :], joined_color], axis=1)
    return (new_tsdf, new_weight)


PLANES = 6
SPANS = ((0, 2), (2, 4), (4, 6))
CHUNKS = len(SPANS)
LANES = 128
LOG = 7
UNROLL = 64
MESH = pl.DeviceIdType.MESH
NT = (((1,), (1,)), ((), ()))
NN = (((1,), (0,)), ((), ()))


def exchange_kernel(
    owners, reps, share,
    counts_ref, bins_ref, table_ref, voxel_hbm, sdf_hbm, weight_hbm, color_hbm,
    out_ref, meta_ref,
    send1, recv1, send2, meta_send1, meta_recv1, meta_send2, meta_recv2,
    s1_send, s1_recv, m1_send, m1_recv, s2_send, s2_recv, m2_send, m2_recv, own_sem,
    voxel_ref, sdf_ref, weight_ref, color_ref, load_sem,
):
    f32, bf16, i32 = jnp.float32, jnp.bfloat16, jnp.int32
    bins = voxel_ref.shape[0]
    capacity = 2 * bins // owners
    slots = owners * capacity
    quota = 2 * bins // reps
    me = lax.axis_index("owner")
    my_rep = lax.axis_index("rep")
    barrier = pltpu.get_barrier_semaphore()
    for k in range(1, owners):
        pl.semaphore_signal(
            barrier, inc=1, device_id=(lax.rem(me + k, owners), my_rep), device_id_type=MESH
        )
    for k in range(1, reps):
        pl.semaphore_signal(
            barrier, inc=1, device_id=(me, lax.rem(my_rep + k, reps)), device_id_type=MESH
        )

    loads = [
        pltpu.make_async_copy(source, target, load_sem.at[i])
        for i, (source, target) in enumerate(
            (
                (weight_hbm, weight_ref),
                (sdf_hbm, sdf_ref),
                (color_hbm, color_ref),
                (voxel_hbm, voxel_ref),
            )
        )
    ]
    for load in loads:
        load.start()

    lane_bin = lax.broadcasted_iota(i32, (capacity, bins), 1)
    row_slot = lax.broadcasted_iota(i32, (capacity, bins), 0)
    picks = []
    start = jnp.int32(0)
    for t in range(owners):
        count = counts_ref[0, t]
        hit = (lane_bin == row_slot + start) & (row_slot < count)
        picks.append(jnp.where(hit, 1.0, 0.0).astype(bf16))
        start = start + count
    pick1 = jnp.concatenate(picks, axis=0)

    ids = bins_ref[...]
    low = lax.broadcasted_iota(i32, (LANES, bins), 0) == (ids & (LANES - 1))
    rows = table_ref.shape[0]
    table = (table_ref[...] & (OWN - 1)).astype(f32).astype(bf16)
    looked = lax.dot_general(
        table, jnp.where(low, 1.0, 0.0).astype(bf16), NN, preferred_element_type=f32
    )
    high = lax.broadcasted_iota(i32, (rows, bins), 0) == lax.shift_right_logical(ids, LOG)
    place = jnp.sum(jnp.where(high, looked, 0.0), axis=0, keepdims=True) + 1.0
    place = jnp.broadcast_to(place, (8, bins)).astype(bf16)
    sent_places = lax.dot_general(place, pick1, NT, preferred_element_type=f32)
    for t in range(slots // LANES):
        meta_send1[t] = sent_places[:, t * LANES : (t + 1) * LANES]

    for load in loads:
        load.wait()
    weight = weight_ref[...]
    wide = weight.astype(f32)
    planes = [(wide * sdf_ref[...].astype(f32)).astype(bf16)]
    for c in range(3):
        planes.append((wide * color_ref[c].astype(f32)).astype(bf16))
    planes.append(weight)
    planes.append((voxel_ref[...] - 256).astype(f32).astype(bf16))

    def span(c):
        return pl.ds(SPANS[c][0], SPANS[c][1] - SPANS[c][0])

    def owner_copy(c, k):
        partner = lax.rem(me + k, owners)
        return pltpu.make_async_remote_copy(
            src_ref=send1.at[span(c), pl.ds(pl.multiple_of(partner * capacity, capacity), capacity)],
            dst_ref=recv1.at[span(c), pl.ds(pl.multiple_of(me * capacity, capacity), capacity)],
            send_sem=s1_send.at[c, k],
            recv_sem=s1_recv.at[c, k],
            device_id=(partner, my_rep),
            device_id_type=MESH,
        )

    def owner_meta(k):
        partner = lax.rem(me + k, owners)
        return pltpu.make_async_remote_copy(
            src_ref=meta_send1.at[partner // 2],
            dst_ref=meta_recv1.at[me],
            send_sem=m1_send.at[k],
            recv_sem=m1_recv.at[k],
            device_id=(partner, my_rep),
            device_id_type=MESH,
        )

    def rep_copy(c, k):
        partner = lax.rem(my_rep + k, reps)
        return pltpu.make_async_remote_copy(
            src_ref=send2.at[span(c), pl.ds(pl.multiple_of(partner * quota, quota), quota)],
            dst_ref=out_ref.at[span(c), pl.ds(pl.multiple_of(my_rep * quota, quota), quota)],
            send_sem=s2_send.at[c, k],
            recv_sem=s2_recv.at[c, k],
            device_id=(me, partner),
            device_id_type=MESH,
        )

    def own_copy(c):
        return pltpu.make_async_copy(
            send2.at[span(c), mine2], out_ref.at[span(c), mine2], own_sem.at[c]
        )

    def rep_meta(k):
        partner = lax.rem(my_rep + k, reps)
        return pltpu.make_async_remote_copy(
            src_ref=meta_send2.at[partner],
            dst_ref=meta_recv2.at[my_rep],
            send_sem=m2_send.at[k],
            recv_sem=m2_recv.at[k],
            device_id=(me, partner),
            device_id_type=MESH,
        )

    for c in range(CHUNKS):
        first, last = SPANS[c]
        data = jnp.concatenate(planes[first:last], axis=1)
        moved = lax.dot_general(pick1, data, NN, preferred_element_type=f32).astype(bf16)
        for p in range(first, last):
            send1[p] = moved[:, (p - first) * LANES : (p - first + 1) * LANES]
        if c == 0:
            pl.semaphore_wait(barrier, owners + reps - 2)
            for k in range(1, owners):
                owner_meta(k).start()
        for k in range(1, owners):
            owner_copy(c, k).start()
    mine = pl.ds(pl.multiple_of(me * capacity, capacity), capacity)
    for p in range(PLANES):
        recv1[p, mine] = send1[p, mine]
    meta_recv1[me] = meta_send1[me // 2]

    before = lax.broadcasted_iota(i32, (slots, slots), 0) < lax.broadcasted_iota(
        i32, (slots, slots), 1
    )
    before = jnp.where(before, 1.0, 0.0).astype(bf16)
    for k in range(1, owners):
        owner_meta(k).wait()
    lane = lax.broadcasted_iota(i32, (8, LANES), 1)
    even = lax.rem(me, 2) == 0
    pieces = []
    for pair in range(owners // 2):
        first, second = meta_recv1[2 * pair], meta_recv1[2 * pair + 1]
        first = jnp.where(even, first, pltpu.roll(first, capacity, 1))
        second = jnp.where(even, pltpu.roll(second, capacity, 1), second)
        pieces.append(jnp.where(lane < capacity, first, second))
    arrived = jnp.concatenate(pieces, axis=1)
    arrived_id = arrived.astype(i32) - 1
    quarter = jnp.where(arrived_id < 0, -1, lax.div(arrived_id, share))
    member = lax.broadcasted_iota(i32, (8, slots), 0) == quarter
    ranks = lax.dot_general(
        jnp.where(member, 1.0, 0.0).astype(bf16), before, NN, preferred_element_type=f32
    )
    rank = jnp.sum(jnp.where(member, ranks, 0.0), axis=0, keepdims=True).astype(i32)
    goal = jnp.where(arrived_id[:1] < 0, -1, quarter[:1] * quota + rank)
    pick2 = jnp.where(lax.broadcasted_iota(i32, (reps * quota, slots), 0) == goal, 1.0, 0.0)
    pick2 = pick2.astype(bf16)
    final_place = jnp.where(arrived_id < 0, 0, lax.rem(arrived_id, share) + 1).astype(f32).astype(bf16)
    final_place = lax.dot_general(final_place, pick2, NT, preferred_element_type=f32)
    for q in range(reps):
        meta_send2[q] = final_place[:, q * quota : (q + 1) * quota]
    mine2 = pl.ds(pl.multiple_of(my_rep * quota, quota), quota)
    for c in range(CHUNKS):
        for k in range(1, owners):
            owner_copy(c, k).wait_recv()
        first, last = SPANS[c]
        data = jnp.concatenate([recv1[p] for p in range(first, last)], axis=1)
        moved = lax.dot_general(pick2, data, NN, preferred_element_type=f32).astype(bf16)
        for p in range(first, last):
            send2[p] = moved[:, (p - first) * LANES : (p - first + 1) * LANES]
        if c == 0:
            for k in range(1, reps):
                rep_meta(k).start()
        for k in range(1, reps):
            rep_copy(c, k).start()
        own_copy(c).start()
    meta_recv2[my_rep] = meta_send2[my_rep]
    for k in range(1, reps):
        rep_meta(k).wait()
    for r in range(reps):
        tile = meta_recv2[r].astype(i32)
        live = jnp.sum(jnp.where(tile > 0, 1.0, 0.0), axis=1, keepdims=True).astype(i32)
        row = lax.broadcasted_iota(i32, (8, quota), 0)
        meta_ref[r] = jnp.where(row == 1, live, jnp.maximum(tile - 1, 0))
    for c in range(CHUNKS):
        for k in range(1, owners):
            owner_copy(c, k).wait_send()
        for k in range(1, reps):
            rep_copy(c, k).wait()
        own_copy(c).wait()


def join_kernel(
    reps, meta_ref, data_ref, tsdf_hbm, oldw_hbm, new_tsdf_ref, new_weight_ref,
    feats, acc, tsdf_ref, oldw_ref, sems,
):
    f32, bf16, i32 = jnp.float32, jnp.bfloat16, jnp.int32
    slots = data_ref.shape[1]
    quota = slots // reps
    blocks, _, cells = tsdf_ref.shape
    uppers = cells // LANES
    copies = [
        pltpu.make_async_copy(tsdf_hbm, tsdf_ref, sems.at[0]),
        pltpu.make_async_copy(oldw_hbm, oldw_ref, sems.at[1]),
    ]
    copies[0].start()
    copies[1].start()
    for p in range(PLANES - 1):
        feats[p * slots : (p + 1) * slots] = data_ref[p].astype(f32)
    voxel = data_ref[PLANES - 1].astype(i32) + 256
    feats[5 * slots : 6 * slots] = (voxel & (LANES - 1)).astype(f32)
    feats[6 * slots : 7 * slots] = lax.shift_right_logical(voxel, LOG).astype(f32)
    feats[7 * slots : 8 * slots] = jnp.zeros((slots, LANES), f32)
    acc[...] = jnp.zeros(acc.shape, f32)
    lower_ids = lax.broadcasted_iota(i32, (LANES, LANES), 0).astype(f32)

    ends = [meta_ref[0, 1, 0]]
    for r in range(1, reps):
        ends.append(ends[-1] + meta_ref[r, 1, 0])

    @pl.loop(0, (ends[-1] + UNROLL - 1) // UNROLL)
    def _(g):
        places, sums = [], []
        for u in range(0, UNROLL, 2):
            rights, lefts = [], []
            for v in range(2):
                flat = g * UNROLL + u + v
                skip = jnp.int32(0)
                before = jnp.int32(0)
                for r in range(reps - 1):
                    skip = jnp.where(flat >= ends[r], (r + 1) * quota, skip)
                    before = jnp.where(flat >= ends[r], ends[r], before)
                slot = jnp.minimum(skip + flat - before, slots - 1)
                keep = flat < ends[-1]
                places.append(jnp.where(keep, meta_ref[lax.shift_right_logical(slot, LOG), 0, slot & (LANES - 1)], blocks))
                x = feats[pl.ds(slot, 8, stride=slots), :]
                rights.append(jnp.where(lower_ids == x[5:6], 1.0, 0.0).astype(bf16))
                lefts.append(
                    jnp.concatenate(
                        [jnp.where(x[6:7] == float(h), x, 0.0) for h in range(uppers)], axis=0
                    ).astype(bf16)
                )
            zero = jnp.zeros_like(lefts[0])
            left = jnp.concatenate(
                [
                    jnp.concatenate([lefts[0], zero], axis=1),
                    jnp.concatenate([zero, lefts[1]], axis=1),
                ],
                axis=0,
            )
            both = lax.dot_general(
                left, jnp.concatenate(rights, axis=1), NT, preferred_element_type=f32
            )
            sums.extend([both[: 8 * uppers], both[8 * uppers :]])
        for place, part in zip(places, sums):
            for h in range(uppers):
                acc[place, :, h * LANES : (h + 1) * LANES] += part[8 * h : 8 * h + 8]

    copies[0].wait()
    copies[1].wait()

    @pl.loop(0, blocks // 8)
    def _(b8):
        base = pl.multiple_of(b8 * 8, 8)
        weights = oldw_ref[pl.ds(base, 8), :]
        news = []
        for i in range(8):
            sums = acc[base + i]
            weight = weights[i : i + 1]
            total = weight + sums[4:5]
            news.append(total)
            new_tsdf_ref[base + i] = (weight * tsdf_ref[base + i] + sums[:4]) / total
        new_weight_ref[pl.ds(base, 8), :] = jnp.concatenate(news, axis=0)


def join_call(reps, meta, data, old_tsdf, old_weight):
    slots = data.shape[1]
    blocks, _, cells = old_tsdf.shape
    vmem = pl.BlockSpec(memory_space=pltpu.VMEM)
    smem = pl.BlockSpec(memory_space=pltpu.SMEM)
    hbm = pl.BlockSpec(memory_space=pl.ANY)
    return pl.pallas_call(
        lambda *refs: join_kernel(reps, *refs),
        out_shape=(
            jax.ShapeDtypeStruct(old_tsdf.shape, jnp.float32),
            jax.ShapeDtypeStruct(old_weight.shape, jnp.float32),
        ),
        in_specs=[smem, vmem, hbm, hbm],
        out_specs=(vmem, vmem),
        scratch_shapes=[
            pltpu.VMEM((8 * slots, LANES), jnp.float32),
            pltpu.VMEM((blocks + 1, 8, cells), jnp.float32),
            pltpu.VMEM(old_tsdf.shape, jnp.float32),
            pltpu.VMEM(old_weight.shape, jnp.float32),
            pltpu.SemaphoreType.DMA((2,)),
        ],
        name="join",
    )(meta, data, old_tsdf, old_weight)


def exchange_call(
    owners, reps, bin_blocks, send_counts, voxel_index, point_sdf, point_weight, point_color,
    owner_table,
):
    bins = voxel_index.shape[0]
    capacity = 2 * bins // owners
    quota = 2 * bins // reps
    slots = owners * capacity
    vmem = pl.BlockSpec(memory_space=pltpu.VMEM)
    smem = pl.BlockSpec(memory_space=pltpu.SMEM)
    dma = pltpu.SemaphoreType.DMA
    return pl.pallas_call(
        lambda *refs: exchange_kernel(owners, reps, OWN // reps, *refs),
        out_shape=(
            jax.ShapeDtypeStruct((PLANES, slots, LANES), jnp.bfloat16),
            jax.ShapeDtypeStruct((reps, 8, LANES), jnp.int32),
        ),
        in_specs=[smem, vmem, vmem] + [pl.BlockSpec(memory_space=pl.ANY)] * 4,
        out_specs=(pl.BlockSpec(memory_space=pl.ANY), vmem),
        scratch_shapes=[
            pltpu.VMEM((PLANES, slots, LANES), jnp.bfloat16),
            pltpu.VMEM((PLANES, slots, LANES), jnp.bfloat16),
            pltpu.VMEM((PLANES, slots, LANES), jnp.bfloat16),
            pltpu.VMEM((slots // LANES, 8, LANES), jnp.float32),
            pltpu.VMEM((owners, 8, LANES), jnp.float32),
            pltpu.VMEM((reps, 8, LANES), jnp.float32),
            pltpu.VMEM((reps, 8, LANES), jnp.float32),
            dma((CHUNKS, owners)),
            dma((CHUNKS, owners)),
            dma((owners,)),
            dma((owners,)),
            dma((CHUNKS, reps)),
            dma((CHUNKS, reps)),
            dma((reps,)),
            dma((reps,)),
            dma((CHUNKS,)),
            pltpu.VMEM(voxel_index.shape, jnp.int32),
            pltpu.VMEM(point_sdf.shape, jnp.bfloat16),
            pltpu.VMEM(point_weight.shape, jnp.bfloat16),
            pltpu.VMEM((3, bins, LANES), jnp.bfloat16),
            dma((4,)),
        ],
        compiler_params=pltpu.CompilerParams(collective_id=0, has_side_effects=True),
        name="exchange",
    )(
        send_counts,
        bin_blocks.reshape(1, bins),
        owner_table.reshape(-1, LANES),
        voxel_index,
        point_sdf,
        point_weight,
        jnp.transpose(point_color, (1, 0, 2)),
    )


def joined(
    bin_blocks,
    send_counts,
    voxel_index,
    point_sdf,
    point_weight,
    point_color,
    owner_table,
    old_tsdf,
    old_weight,
):
    owners, reps = lax.axis_size("owner"), lax.axis_size("rep")
    bins, points = voxel_index.shape
    capacity = 2 * bins // owners
    quota = 2 * bins // reps
    if 2 * capacity != LANES or quota != LANES or points != LANES:
        return local(
            bin_blocks, send_counts, voxel_index, point_sdf, point_weight, point_color,
            owner_table, old_tsdf, old_weight,
        )
    data, meta = exchange_call(
        owners, reps, bin_blocks, send_counts, voxel_index, point_sdf, point_weight, point_color,
        owner_table,
    )
    return join_call(reps, meta, data, old_tsdf, old_weight)


def solution(mesh):
    placed = (
        P(("owner", "rep")),
        P(("owner", "rep"), None),
        P(("owner", "rep"), None),
        P(("owner", "rep"), None),
        P(("owner", "rep"), None),
        P(("owner", "rep"), None, None),
        P(),
        P(("owner", "rep"), None, None),
        P(("owner", "rep"), None),
    )
    return jax.shard_map(
        joined,
        mesh=mesh,
        in_specs=placed,
        out_specs=(P(("owner", "rep"), None, None), P(("owner", "rep"), None)),
        check_vma=False,
    )
```

profile of v0, /device:TPU:0, one launch (start us, length us, event | category | flops | bytes accessed | tf_op | source)
XLA Modules:
  0.0 37.6 jit_solution(3433158087635298607)
XLA Ops:
  0.6 30.2 %exchange.1 = (bf16[6,512,128]{2,1,0:T(8,128)(2,1)}, s32[4,8,128]{2,1,0:T(8,128)}) custom-call(s32[1,8]{1,0:T(1,128)} %refs_0_.1, s32[1,256]{1,0:T(1,128)} %bitcast.5, s32[16,128]{1,0:T(8,128)} %bitcast.4, s32[256,128]{1,0:T(8,128)} %refs_3_.2, bf16[256,128]{1,0:T(8,128)(2,1)} %refs_4_.1, bf16[256,128]{1,0:T(8,128)(2,1)} %refs_5_.1, bf16[3,256,128]{2,1,0:T(8,128)(2,1)} %bitcast.3), custom_call_target="tpu_custom_call" | custom-call | tf_op jit(solution)/shard_map/exchange/pallas_call | solution.py:462
  30.9 6.7 %join.1 = (f32[64,4,512]{2,1,0:T(4,128)}, f32[64,512]{1,0:T(8,128)}) custom-call(s32[4,8,128]{2,1,0:T(8,128)} %get-tuple-element.4.refs_0_, bf16[6,512,128]{2,1,0:T(8,128)(2,1)} %get-tuple-element.5.refs_1_, f32[64,4,512]{2,1,0:T(4,128)} %refs_2_.1, f32[64,512]{1,0:T(8,128)} %refs_3_.3), custom_call_target="tpu_custom_call" | custom-call | tf_op jit(solution)/shard_map/join/pallas_call | solution.py:432
where the time goes:
time: 37.7 us; the launch traced here: 37.6 us
  Pallas kernels  37 us (98%)
  between operations  0.64 us (2%)
    pallas_call x1, Pallas kernels, exchange_call(): pl.pallas_call(lambda *refs: exchange_kernel(owners, reps, OWN // reps, *...  30.2 us
    pallas_call x1, Pallas kernels, join_call(): pl.pallas_call(lambda *refs: join_kernel(reps, *refs), out_shape=(jax.Sha...  6.73 us

commit v1 on v0

v1 whole, which is shorter than its diff:
```python
import math

import jax
import jax.numpy as jnp
from jax import lax
from jax.experimental import pallas as pl
from jax.experimental.pallas import tpu as pltpu
from jax.sharding import PartitionSpec as P

OWN = 256
VA = 8
VB = 64


def accumulate(feature_list, voxels, block_rows, block_total):
    slot_count, points = voxels.shape
    group_size = math.gcd(slot_count, 128)
    group_count = slot_count // group_size
    channels = sum_channels(feature_list)
    grouped = tuple((f.reshape((group_count, group_size) + f.shape[1:]) for f in feature_list))
    voxel_groups = voxels.reshape(group_count, group_size, points)
    block_groups = jnp.maximum(block_rows, 0).reshape(group_count, group_size)
    upper_ids = jnp.arange(VA, dtype=jnp.int32)
    lower_ids = jnp.arange(VB, dtype=jnp.int32)

    def fold_group(running, pieces):
        feature_parts, voxel_rows, block_ids = pieces
        features_group = jnp.concatenate(list(feature_parts), axis=1)
        upper_part = voxel_rows // VB
        lower_part = voxel_rows % VB
        chosen = upper_part[:, None, :] == upper_ids[None, :, None]
        left_side = jnp.where(
            chosen[:, None], features_group[:, :, None, :], jnp.zeros((), jnp.bfloat16)
        )
        left_side = left_side.reshape(group_size, channels * VA, points)
        right_side = (lower_part[:, :, None] == lower_ids[None, None, :]).astype(jnp.bfloat16)
        slot_grids = jnp.einsum(
            "gkp,gpb->gkb", left_side, right_side, preferred_element_type=jnp.float32
        )
        slot_grids = slot_grids.reshape(group_size, channels, VA * VB)
        return (running.at[block_ids].add(slot_grids), None)

    running_start = jnp.zeros((block_total, channels, VA * VB), jnp.float32)
    running_end, _ = lax.scan(fold_group, running_start, (grouped, voxel_groups, block_groups))
    return running_end


def sum_channels(feature_list):
    total_channels = 0
    for member in feature_list:
        total_channels = total_channels + member.shape[1]
    return total_channels


def local(
    bin_blocks,
    send_counts,
    voxel_index,
    point_sdf,
    point_weight,
    point_color,
    owner_table,
    old_tsdf,
    old_weight,
):
    owners = lax.axis_size("owner")
    bin_count = bin_blocks.shape[0]
    capacity = 2 * bin_count // owners
    slot_count = owners * capacity
    counts = send_counts[0]
    starts = jnp.cumsum(counts) - counts
    slot_ids = jnp.arange(slot_count, dtype=jnp.int32)
    target = slot_ids // capacity
    position = slot_ids % capacity
    active = position < counts[target]
    source = jnp.clip(starts[target] + position, 0, bin_count - 1)
    blocks_sent = jnp.where(active, owner_table[bin_blocks[source]] % OWN, -1)
    weight = jnp.where(active[:, None], point_weight[source], jnp.zeros((), jnp.bfloat16))
    wide_weight = weight.astype(jnp.float32)
    weighted_sdf = (wide_weight * point_sdf[source].astype(jnp.float32)).astype(jnp.bfloat16)
    geometry = jnp.stack([weight, weighted_sdf], axis=1)
    colors = (wide_weight[:, None, :] * point_color[source].astype(jnp.float32)).astype(
        jnp.bfloat16
    )
    voxels = voxel_index[source]
    replicas = lax.axis_size("rep")
    share = OWN // replicas
    arrived_geometry, arrived_colors, arrived_voxels, arrived_blocks = (
        lax.all_to_all(geometry, "owner", split_axis=0, concat_axis=0, tiled=True),
        lax.all_to_all(colors, "owner", split_axis=0, concat_axis=0, tiled=True),
        lax.all_to_all(voxels, "owner", split_axis=0, concat_axis=0, tiled=True),
        lax.all_to_all(blocks_sent, "owner", split_axis=0, concat_axis=0, tiled=True),
    )
    quota = 2 * bin_count // replicas
    live = arrived_blocks >= 0
    quarter = jnp.where(live, arrived_blocks // share, 0)
    quarter_ids = jnp.arange(replicas, dtype=jnp.int32)
    member = (live[:, None] & (quarter[:, None] == quarter_ids[None, :])).astype(jnp.int32)
    rank = jnp.sum((jnp.cumsum(member, axis=0) - member) * member, axis=1)
    outgoing_slots = replicas * quota
    destination = jnp.where(live, quarter * quota + rank, outgoing_slots).astype(jnp.int32)
    arrived_ids = jnp.arange(arrived_blocks.shape[0], dtype=jnp.int32)
    picked = jnp.zeros((outgoing_slots,), jnp.int32).at[destination].set(arrived_ids, mode="drop")
    filled = jnp.zeros((outgoing_slots,), jnp.bool_).at[destination].set(True, mode="drop")
    send_geometry = jnp.where(
        filled[:, None, None], arrived_geometry[picked], jnp.zeros((), jnp.bfloat16)
    )
    send_colors = jnp.where(
        filled[:, None, None], arrived_colors[picked], jnp.zeros((), jnp.bfloat16)
    )
    send_voxels = arrived_voxels[picked]
    send_places = jnp.where(filled, arrived_blocks[picked] % share, -1).astype(jnp.int32)
    final_geometry, final_colors, final_voxels, final_places = (
        lax.all_to_all(send_geometry, "rep", split_axis=0, concat_axis=0, tiled=True),
        lax.all_to_all(send_colors, "rep", split_axis=0, concat_axis=0, tiled=True),
        lax.all_to_all(send_voxels, "rep", split_axis=0, concat_axis=0, tiled=True),
        lax.all_to_all(send_places, "rep", split_axis=0, concat_axis=0, tiled=True),
    )
    cell_sums = accumulate((final_geometry, final_colors), final_voxels, final_places, share)
    geometry_share = cell_sums[:, :2]
    color_share = cell_sums[:, 2:]
    new_weight = old_weight + geometry_share[:, 0]
    joined_sdf = (old_weight * old_tsdf[:, 0] + geometry_share[:, 1]) / new_weight
    joined_color = (old_weight[:, None, :] * old_tsdf[:, 1:] + color_share) / new_weight[:, None, :]
    new_tsdf = jnp.concatenate([joined_sdf[:, None, :], joined_color], axis=1)
    return (new_tsdf, new_weight)


PLANES = 6
COLORS = 3
LANES = 128
LOG = 7
UPPERS = 8
LOWERS = 64
UNROLL = 64
FAR = (4, 5, 6, 7)
NEAR = (2, 3, 1)
GROUPS = ((0,), (1,), (2,), (3,), (4,), (5,))
MESH = pl.DeviceIdType.MESH
NT = (((1,), (1,)), ((), ()))
NN = (((1,), (0,)), ((), ()))


def mirrored(index, bits):
    bit = 1
    while bit <= bits:
        if bits & bit:
            index = index + bit * (1 - 2 * lax.rem(lax.div(index, bit), 2))
        bit *= 2
    return index


def exchange_kernel(
    owners, reps, share,
    counts_hbm, bins_hbm, table_hbm, voxel_hbm, sdf_hbm, weight_hbm, color_hbm,
    feats_ref, meta_ref,
    send1, recv1, send2, final, pick2_ref, meta_send1, meta_recv1, meta_send2, meta_recv2, listed,
    s1_send, s1_recv, m1_send, m1_recv, s2_send, s2_recv, m2_send, m2_recv,
    counts_ref, bins_ref, table_ref, voxel_ref, sdf_ref, weight_ref, color_ref, load_sem,
):
    f32, bf16, i32 = jnp.float32, jnp.bfloat16, jnp.int32
    bins = voxel_ref.shape[0]
    capacity = 2 * bins // owners
    slots = owners * capacity
    quota = 2 * bins // reps
    me = lax.axis_index("owner")
    my_rep = lax.axis_index("rep")
    barrier = pltpu.get_barrier_semaphore()
    for k in FAR + NEAR:
        pl.semaphore_signal(barrier, inc=1, device_id=(mirrored(me, k), my_rep), device_id_type=MESH)
    for k in range(1, reps):
        pl.semaphore_signal(
            barrier, inc=1, device_id=(me, mirrored(my_rep, k)), device_id_type=MESH
        )

    loads = [
        pltpu.make_async_copy(source, target, load_sem.at[i])
        for i, (source, target) in enumerate(
            (
                (counts_hbm, counts_ref),
                (voxel_hbm, voxel_ref),
                (bins_hbm, bins_ref),
                (table_hbm, table_ref),
                (weight_hbm, weight_ref),
                (sdf_hbm, sdf_ref),
                (color_hbm, color_ref),
            )
        )
    ]
    for load in loads:
        load.start()

    def owner_copy(p, k):
        partner = mirrored(me, k)
        return pltpu.make_async_remote_copy(
            src_ref=send1.at[p, pl.ds(pl.multiple_of(partner * capacity, capacity), capacity)],
            dst_ref=recv1.at[p, pl.ds(pl.multiple_of(me * capacity, capacity), capacity)],
            send_sem=s1_send.at[p, k],
            recv_sem=s1_recv.at[p, k],
            device_id=(partner, my_rep),
            device_id_type=MESH,
        )

    def owner_meta(k):
        partner = mirrored(me, k)
        return pltpu.make_async_remote_copy(
            src_ref=meta_send1.at[lax.div(partner, 2)],
            dst_ref=meta_recv1.at[me],
            send_sem=m1_send.at[k],
            recv_sem=m1_recv.at[k],
            device_id=(partner, my_rep),
            device_id_type=MESH,
        )

    def quarter_rows(q):
        return pl.ds(pl.multiple_of(q * quota, quota), quota)

    def rep_copy(p, k):
        partner = mirrored(my_rep, k)
        return pltpu.make_async_remote_copy(
            src_ref=send2.at[p, quarter_rows(partner)],
            dst_ref=final.at[p, quarter_rows(my_rep)],
            send_sem=s2_send.at[p, k],
            recv_sem=s2_recv.at[p, k],
            device_id=(me, partner),
            device_id_type=MESH,
        )

    def rep_meta(k):
        partner = mirrored(my_rep, k)
        return pltpu.make_async_remote_copy(
            src_ref=meta_send2.at[partner],
            dst_ref=meta_recv2.at[my_rep],
            send_sem=m2_send.at[k],
            recv_sem=m2_recv.at[k],
            device_id=(me, partner),
            device_id_type=MESH,
        )

    lane_bin = lax.broadcasted_iota(i32, (capacity, bins), 1)
    row_slot = lax.broadcasted_iota(i32, (capacity, bins), 0)
    loads[0].wait()
    picks = []
    start = jnp.int32(0)
    for t in range(owners):
        count = counts_ref[0, t]
        hit = (lane_bin == row_slot + start) & (row_slot < count)
        picks.append(jnp.where(hit, 1.0, 0.0).astype(bf16))
        start = start + count
    pick1 = jnp.concatenate(picks, axis=0)

    inner = lax.rem(lax.div(lax.div(me, 2) + 1, 2), 2)

    def send_plane(p, data):
        send1[p] = lax.dot_general(pick1, data, NN, preferred_element_type=f32).astype(bf16)
        if p == 0:
            pl.semaphore_wait(barrier, owners + reps - 2)
        for k in FAR[:2]:
            owner_copy(p, k).start()

        @pl.when(inner == 0)
        def _():
            for k in FAR[2:]:
                owner_copy(p, k).start()

        for k in NEAR:
            owner_copy(p, k).start()

        for group in GROUPS:
            if group[-1] == p:

                @pl.when(inner == 1)
                def _():
                    for late in group:
                        for k in FAR[2:]:
                            owner_copy(late, k).start()

    loads[1].wait()
    send_plane(0, (voxel_ref[...] - 256).astype(f32).astype(bf16))

    loads[2].wait()
    loads[3].wait()
    ids = bins_ref[...]
    low = lax.broadcasted_iota(i32, (LANES, bins), 0) == (ids & (LANES - 1))
    rows = table_ref.shape[0]
    table = (table_ref[...] & (OWN - 1)).astype(f32).astype(bf16)
    looked = lax.dot_general(
        table, jnp.where(low, 1.0, 0.0).astype(bf16), NN, preferred_element_type=f32
    )
    high = lax.broadcasted_iota(i32, (rows, bins), 0) == lax.shift_right_logical(ids, LOG)
    place = jnp.sum(jnp.where(high, looked, 0.0), axis=0, keepdims=True) + 1.0
    place = jnp.broadcast_to(place, (8, bins)).astype(bf16)
    sent_places = lax.dot_general(place, pick1, NT, preferred_element_type=f32)
    for t in range(slots // LANES):
        meta_send1[t] = sent_places[:, t * LANES : (t + 1) * LANES]
    for k in FAR + NEAR:
        owner_meta(k).start()

    loads[4].wait()
    weight = weight_ref[...]
    wide = weight.astype(f32)
    send_plane(1, weight)
    loads[5].wait()
    send_plane(2, (wide * sdf_ref[...].astype(f32)).astype(bf16))
    loads[6].wait()
    for c in range(COLORS):
        send_plane(3 + c, (wide * color_ref[c].astype(f32)).astype(bf16))

    mine = pl.ds(pl.multiple_of(me * capacity, capacity), capacity)
    for p in range(PLANES):
        recv1[p, mine] = send1[p, mine]
    meta_recv1[me] = meta_send1[lax.div(me, 2)]

    before = lax.broadcasted_iota(i32, (slots, slots), 0) < lax.broadcasted_iota(
        i32, (slots, slots), 1
    )
    before = jnp.where(before, 1.0, 0.0).astype(bf16)
    for k in FAR + NEAR:
        owner_meta(k).wait()
    lane = lax.broadcasted_iota(i32, (8, LANES), 1)
    even = lax.rem(me, 2) == 0
    pieces = []
    for pair in range(owners // 2):
        first, second = meta_recv1[2 * pair], meta_recv1[2 * pair + 1]
        first = jnp.where(even, first, pltpu.roll(first, capacity, 1))
        second = jnp.where(even, pltpu.roll(second, capacity, 1), second)
        pieces.append(jnp.where(lane < capacity, first, second))
    arrived = jnp.concatenate(pieces, axis=1)
    arrived_id = arrived.astype(i32) - 1
    quarter = jnp.where(arrived_id < 0, -1, lax.div(arrived_id, share))
    member = lax.broadcasted_iota(i32, (8, slots), 0) == quarter
    ranks = lax.dot_general(
        jnp.where(member, 1.0, 0.0).astype(bf16), before, NN, preferred_element_type=f32
    )
    rank = jnp.sum(jnp.where(member, ranks, 0.0), axis=0, keepdims=True).astype(i32)
    goal = jnp.where(arrived_id[:1] < 0, -1, quarter[:1] * quota + rank)
    pick2 = jnp.where(lax.broadcasted_iota(i32, (reps * quota, slots), 0) == goal, 1.0, 0.0)
    pick2 = pick2.astype(bf16)
    pick2_ref[...] = pick2
    final_place = jnp.where(arrived_id < 0, 0, lax.rem(arrived_id, share) + 1).astype(f32).astype(bf16)
    final_place = lax.dot_general(final_place, pick2, NT, preferred_element_type=f32)
    for q in range(reps):
        meta_send2[q] = final_place[:, q * quota : (q + 1) * quota]
    for k in range(1, reps):
        rep_meta(k).start()
    meta_recv2[my_rep] = meta_send2[my_rep]

    def relay(p):
        for k in FAR + NEAR:
            owner_copy(p, k).wait_recv()
        data = recv1[p]
        for k in (2, 3, 1):
            q = quarter_rows(mirrored(my_rep, k))
            send2[p, q] = lax.dot_general(
                pick2_ref[q], data, NN, preferred_element_type=f32
            ).astype(bf16)
            rep_copy(p, k).start()
        q = quarter_rows(my_rep)
        final[p, q] = lax.dot_general(pick2_ref[q], data, NN, preferred_element_type=f32).astype(bf16)

    def land(p):
        for k in range(1, reps):
            rep_copy(p, k).wait_recv()
        data = final[p].astype(f32)
        if p > 0:
            feats_ref[pl.ds(p - 1, slots, stride=8), :] = data
        else:
            voxel = data.astype(i32) + 256
            feats_ref[pl.ds(5, slots, stride=8), :] = (voxel & (LOWERS - 1)).astype(f32)
            feats_ref[pl.ds(6, slots, stride=8), :] = lax.shift_right_logical(voxel, 6).astype(f32)

    def list_slots():
        for k in range(1, reps):
            rep_meta(k).wait()
        lane = lax.broadcasted_iota(i32, (8, LANES), 1)
        row = lax.broadcasted_iota(i32, (8, LANES), 0)
        targets, values = [], []
        start = jnp.zeros((1, 1), f32)
        for r in range(reps):
            tile = meta_recv2[r]
            live = tile[:1] > 0
            targets.append(jnp.where(live, lane[:1].astype(f32) + start, -1.0))
            values.append(
                jnp.where(row == 0, float(r), jnp.where(row == 1, lane.astype(f32), tile))
            )
            start = start + jnp.sum(jnp.where(live, 1.0, 0.0), axis=1, keepdims=True)
        target = jnp.concatenate(targets, axis=1).astype(i32)
        chosen = lax.broadcasted_iota(i32, (slots, slots), 0) == target
        found = lax.dot_general(
            jnp.concatenate(values, axis=1).astype(bf16),
            jnp.where(chosen, 1.0, 0.0).astype(bf16),
            NT, preferred_element_type=f32,
        )
        base = ((found[:1] * float(quota) + found[1:2]) * 8.0).astype(i32)
        spot = found[2:3].astype(i32)
        spot = jnp.where(spot > 0, spot - 1, share)
        groups = slots // UNROLL
        for g in range(groups):
            part = pl.ds((g * UNROLL) // LANES * LANES, LANES)
            shift = (LANES - (g * UNROLL) % LANES) % LANES
            for source, place in ((base, g), (spot, groups + g)):
                tile = source[:, part.start : part.start + LANES]
                if shift:
                    tile = pltpu.roll(jnp.broadcast_to(tile, (8, LANES)), shift, 1)[:1]
                listed[place : place + 1] = tile
        listed[2 * groups : 2 * groups + 1] = jnp.broadcast_to(start.astype(i32), (1, LANES))
        copy = pltpu.make_async_copy(listed, meta_ref, load_sem.at[0])
        copy.start()
        return copy

    copy = None
    for p in range(PLANES):
        relay(p)
        if p == 1:
            copy = list_slots()
        if p >= 2:
            land(p - 2)
    land(PLANES - 2)
    land(PLANES - 1)
    copy.wait()
    for p in range(PLANES):
        for k in FAR + NEAR:
            owner_copy(p, k).wait_send()
        for k in range(1, reps):
            rep_copy(p, k).wait_send()


def join_kernel(
    meta_ref, feats, tsdf_hbm, oldw_hbm, new_tsdf_ref, new_weight_ref, acc, tsdf_ref, oldw_ref, sems,
):
    f32, bf16, i32 = jnp.float32, jnp.bfloat16, jnp.int32
    blocks, channels, cells = tsdf_ref.shape
    planes = channels + 1
    copies = [
        pltpu.make_async_copy(tsdf_hbm, tsdf_ref, sems.at[0]),
        pltpu.make_async_copy(oldw_hbm, oldw_ref, sems.at[1]),
    ]
    copies[0].start()
    copies[1].start()
    groups = feats.shape[0] // 8 // UNROLL
    acc[...] = jnp.zeros(acc.shape, f32)
    lower_ids = lax.broadcasted_iota(i32, (LOWERS, LANES), 0).astype(f32).astype(bf16)
    upper_ids = lax.broadcasted_iota(i32, (UPPERS, LANES), 0).astype(f32)
    empty = jnp.zeros((planes * UPPERS, LANES), f32)

    @pl.loop(0, lax.div(meta_ref[2 * groups, 0] + (UNROLL - 1), UNROLL))
    def _(g):
        for u in range(0, UNROLL, 2):
            rights, lefts, places = [], [], []
            for v in range(2):
                base = meta_ref[g, u + v]
                places.append(meta_ref[groups + g, u + v])
                lower = feats[pl.ds(base + 5, 1), :].astype(bf16)
                upper = feats[pl.ds(base + 6, 1), :]
                rights.append(jnp.where(lower_ids == lower, bf16(1), bf16(0)))
                hit = upper_ids == upper
                lefts.append(
                    jnp.concatenate(
                        [jnp.where(hit, feats[pl.ds(base + c, 1), :], 0.0) for c in range(planes)],
                        axis=0,
                    )
                )
            left = jnp.concatenate(
                [
                    jnp.concatenate([lefts[0], empty], axis=0),
                    jnp.concatenate([empty, lefts[1]], axis=0),
                ],
                axis=1,
            ).astype(bf16)
            both = lax.dot_general(
                left, jnp.concatenate(rights, axis=1), NT, preferred_element_type=f32
            )
            for v in range(2):
                rows = pl.ds(0, planes * UPPERS)
                acc[places[v], :, :LOWERS] += both[v * planes * UPPERS : (v + 1) * planes * UPPERS]

    copies[0].wait()
    copies[1].wait()
    lane = lax.broadcasted_iota(i32, (8, LANES), 1)

    @pl.loop(0, blocks // 8)
    def _(b8):
        base = pl.multiple_of(b8 * 8, 8)
        for h in range(cells // LANES):
            span = slice(h * LANES, (h + 1) * LANES)
            weights = oldw_ref[pl.ds(base, 8), span]
            news = []
            for i in range(8):
                even = acc[base + i, pl.ds(2 * h, planes, stride=UPPERS), :]
                odd = acc[base + i, pl.ds(2 * h + 1, planes, stride=UPPERS), :]
                sums = jnp.where(lane[:planes] < LOWERS, even, pltpu.roll(odd, LOWERS, 1))
                weight = weights[i : i + 1]
                total = weight + sums[:1]
                news.append(total)
                new_tsdf_ref[base + i, :, span] = (
                    weight * tsdf_ref[base + i, :, span] + sums[1:]
                ) / total
            new_weight_ref[pl.ds(base, 8), span] = jnp.concatenate(news, axis=0)


def join_call(meta, feats, old_tsdf, old_weight):
    blocks, channels, cells = old_tsdf.shape
    vmem = pl.BlockSpec(memory_space=pltpu.VMEM)
    smem = pl.BlockSpec(memory_space=pltpu.SMEM)
    hbm = pl.BlockSpec(memory_space=pl.ANY)
    return pl.pallas_call(
        join_kernel,
        out_shape=(
            jax.ShapeDtypeStruct(old_tsdf.shape, jnp.float32),
            jax.ShapeDtypeStruct(old_weight.shape, jnp.float32),
        ),
        in_specs=[smem, vmem, hbm, hbm],
        out_specs=(vmem, vmem),
        scratch_shapes=[
            pltpu.VMEM((blocks + 1, (channels + 1) * UPPERS, LANES), jnp.float32),
            pltpu.VMEM(old_tsdf.shape, jnp.float32),
            pltpu.VMEM(old_weight.shape, jnp.float32),
            pltpu.SemaphoreType.DMA((2,)),
        ],
        name="join",
    )(
        pltpu.with_memory_space_constraint(meta, pltpu.SMEM),
        pltpu.with_memory_space_constraint(feats, pltpu.VMEM),
        old_tsdf,
        old_weight,
    )


def exchange_call(
    owners, reps, bin_blocks, send_counts, voxel_index, point_sdf, point_weight, point_color,
    owner_table,
):
    bins = voxel_index.shape[0]
    capacity = 2 * bins // owners
    slots = owners * capacity
    table = owner_table.reshape(-1, LANES)
    vmem = pl.BlockSpec(memory_space=pltpu.VMEM)
    smem = pl.BlockSpec(memory_space=pltpu.SMEM)
    dma = pltpu.SemaphoreType.DMA
    listing = (2 * (slots // UNROLL) + 8, LANES)
    return pl.pallas_call(
        lambda *refs: exchange_kernel(owners, reps, OWN // reps, *refs),
        out_shape=(
            pltpu.VMEM((8 * slots, LANES), jnp.float32),
            pltpu.SMEM(listing, jnp.int32),
        ),
        in_specs=[pl.BlockSpec(memory_space=pl.ANY)] * 7,
        out_specs=(vmem, smem),
        scratch_shapes=[
            pltpu.VMEM((PLANES, slots, LANES), jnp.bfloat16),
            pltpu.VMEM((PLANES, slots, LANES), jnp.bfloat16),
            pltpu.VMEM((PLANES, slots, LANES), jnp.bfloat16),
            pltpu.VMEM((PLANES, slots, LANES), jnp.bfloat16),
            pltpu.VMEM((slots, slots), jnp.bfloat16),
            pltpu.VMEM((slots // LANES, 8, LANES), jnp.float32),
            pltpu.VMEM((owners, 8, LANES), jnp.float32),
            pltpu.VMEM((reps, 8, LANES), jnp.float32),
            pltpu.VMEM((reps, 8, LANES), jnp.float32),
            pltpu.VMEM(listing, jnp.int32),
            dma((PLANES, owners)),
            dma((PLANES, owners)),
            dma((owners,)),
            dma((owners,)),
            dma((PLANES, reps)),
            dma((PLANES, reps)),
            dma((reps,)),
            dma((reps,)),
            pltpu.SMEM(send_counts.shape, jnp.int32),
            pltpu.VMEM((1, bins), jnp.int32),
            pltpu.VMEM(table.shape, jnp.int32),
            pltpu.VMEM(voxel_index.shape, jnp.int32),
            pltpu.VMEM(point_sdf.shape, jnp.bfloat16),
            pltpu.VMEM(point_weight.shape, jnp.bfloat16),
            pltpu.VMEM((COLORS, bins, LANES), jnp.bfloat16),
            dma((7,)),
        ],
        compiler_params=pltpu.CompilerParams(collective_id=0, has_side_effects=True),
        name="exchange",
    )(
        send_counts,
        bin_blocks.reshape(1, bins),
        table,
        voxel_index,
        point_sdf,
        point_weight,
        jnp.transpose(point_color, (1, 0, 2)),
    )


def joined(
    bin_blocks,
    send_counts,
    voxel_index,
    point_sdf,
    point_weight,
    point_color,
    owner_table,
    old_tsdf,
    old_weight,
):
    owners, reps = lax.axis_size("owner"), lax.axis_size("rep")
    bins, points = voxel_index.shape
    capacity = 2 * bins // owners
    quota = 2 * bins // reps
    if owners != 8 or reps != 4 or bins != 256 or points != LANES:
        return local(
            bin_blocks, send_counts, voxel_index, point_sdf, point_weight, point_color,
            owner_table, old_tsdf, old_weight,
        )
    feats, meta = exchange_call(
        owners, reps, bin_blocks, send_counts, voxel_index, point_sdf, point_weight, point_color,
        owner_table,
    )
    return join_call(meta, feats, old_tsdf, old_weight)


def solution(mesh):
    placed = (
        P(("owner", "rep")),
        P(("owner", "rep"), None),
        P(("owner", "rep"), None),
        P(("owner", "rep"), None),
        P(("owner", "rep"), None),
        P(("owner", "rep"), None, None),
        P(),
        P(("owner", "rep"), None, None),
        P(("owner", "rep"), None),
    )
    return jax.shard_map(
        joined,
        mesh=mesh,
        in_specs=placed,
        out_specs=(P(("owner", "rep"), None, None), P(("owner", "rep"), None)),
        check_vma=False,
    )
```

time: 37.7 us -> 35.1 us (0.931)
  Pallas kernels: 37 us -> 34.3 us
    pallas_call x1, Pallas kernels: 6.73 us -> 4.64 us  [join_call(): pl.pallas_call(join_kernel, out_shape=(jax.ShapeDtypeStruct(old_tsdf.shap...]
    pallas_call x1, Pallas kernels: 30.2 us -> 29.6 us  [exchange_call(): pl.pallas_call(lambda *refs: exchange_kernel(owners, reps, OWN // reps, *...]
where the time goes in v1:
time: 35.1 us; the launch traced here: 34.9 us
  Pallas kernels  34.3 us (98%)
  between operations  0.64 us (2%)
    pallas_call x1, Pallas kernels, exchange_call(): pl.pallas_call(lambda *refs: exchange_kernel(owners, reps, OWN // reps, *...  29.6 us
    pallas_call x1, Pallas kernels, join_call(): pl.pallas_call(join_kernel, out_shape=(jax.ShapeDtypeStruct(old_tsdf.shap...  4.64 us

profile of v1, /device:TPU:0, one launch (start us, length us, event | category | flops | bytes accessed | tf_op | source)
XLA Modules:
  0.0 34.9 jit_solution(15256602225944340271)
XLA Ops:
  0.6 29.6 %exchange.1 = (f32[4096,128]{1,0:T(8,128)S(1)}, s32[24,128]{1,0:T(8,128)S(4)}) custom-call(s32[1,8]{1,0:T(1,128)} %refs_0_.1, s32[1,256]{1,0:T(1,128)} %bitcast.5, s32[16,128]{1,0:T(8,128)} %bitcast.4, s32[256,128]{1,0:T(8,128)} %refs_3_.1, bf16[256,128]{1,0:T(8,128)(2,1)} %refs_4_.1, bf16[256,128]{1,0:T(8,128)(2,1)} %refs_5_.1, bf16[3,256,128]{2,1,0:T(8,128)(2,1)} %bitcast.3), custom_call_target="tpu_custom_call" | custom-call | tf_op jit(solution)/shard_map/exchange/pallas_call | solution.py:541
  30.3 4.6 %join.1 = (f32[64,4,512]{2,1,0:T(4,128)}, f32[64,512]{1,0:T(8,128)}) custom-call(s32[24,128]{1,0:T(8,128)S(4)} %get-tuple-element.4.meta_ref, f32[4096,128]{1,0:T(8,128)S(1)} %get-tuple-element.5.feats, f32[64,4,512]{2,1,0:T(4,128)} %tsdf_hbm.1, f32[64,512]{1,0:T(8,128)} %oldw_hbm.1), custom_call_target="tpu_custom_call" | custom-call | tf_op jit(solution)/shard_map/join/pallas_call | solution.py:506

commit v2 on v1

--- a/solution.py
+++ b/solution.py
@@ -135,7 +135,7 @@
 UNROLL = 64
 FAR = (4, 5, 6, 7)
 NEAR = (2, 3, 1)
-GROUPS = ((0,), (1,), (2,), (3,), (4,), (5,))
+LAG = 2
 MESH = pl.DeviceIdType.MESH
 NT = (((1,), (1,)), ((), ()))
 NN = (((1,), (0,)), ((), ()))
@@ -190,24 +190,29 @@
     for load in loads:
         load.start()
 
-    def owner_copy(p, k):
-        partner = mirrored(me, k)
+    def owner_copy(p, partner):
         return pltpu.make_async_remote_copy(
             src_ref=send1.at[p, pl.ds(pl.multiple_of(partner * capacity, capacity), capacity)],
             dst_ref=recv1.at[p, pl.ds(pl.multiple_of(me * capacity, capacity), capacity)],
-            send_sem=s1_send.at[p, k],
-            recv_sem=s1_recv.at[p, k],
+            send_sem=s1_send,
+            recv_sem=s1_recv.at[p],
             device_id=(partner, my_rep),
             device_id_type=MESH,
         )
+
+    def took(bytes_of, semaphore):
+        pltpu.make_async_copy(bytes_of, bytes_of, semaphore).wait()
+
+    def send_copy(p, partner):
+        owner_copy(p, partner).start()
 
     def owner_meta(k):
         partner = mirrored(me, k)
         return pltpu.make_async_remote_copy(
             src_ref=meta_send1.at[lax.div(partner, 2)],
             dst_ref=meta_recv1.at[me],
-            send_sem=m1_send.at[k],
-            recv_sem=m1_recv.at[k],
+            send_sem=m1_send,
+            recv_sem=m1_recv,
             device_id=(partner, my_rep),
             device_id_type=MESH,
         )
@@ -220,8 +225,8 @@
         return pltpu.make_async_remote_copy(
             src_ref=send2.at[p, quarter_rows(partner)],
             dst_ref=final.at[p, quarter_rows(my_rep)],
-            send_sem=s2_send.at[p, k],
-            recv_sem=s2_recv.at[p, k],
+            send_sem=s2_send,
+            recv_sem=s2_recv.at[p // (PLANES - 1)],
             device_id=(me, partner),
             device_id_type=MESH,
         )
@@ -231,8 +236,8 @@
         return pltpu.make_async_remote_copy(
             src_ref=meta_send2.at[partner],
             dst_ref=meta_recv2.at[my_rep],
-            send_sem=m2_send.at[k],
-            recv_sem=m2_recv.at[k],
+            send_sem=m2_send,
+            recv_sem=m2_recv,
             device_id=(me, partner),
             device_id_type=MESH,
         )
@@ -249,31 +254,25 @@
         start = start + count
     pick1 = jnp.concatenate(picks, axis=0)
 
-    inner = lax.rem(lax.div(lax.div(me, 2) + 1, 2), 2)
+    half = owners // 2
+    upper_half = lax.div(me, half)
+    across = (1 - upper_half) * (me + half)
+    far = [mirrored(across, j) for j in range(half)]
+    near = [mirrored(me, k) for k in NEAR]
 
     def send_plane(p, data):
         send1[p] = lax.dot_general(pick1, data, NN, preferred_element_type=f32).astype(bf16)
         if p == 0:
             pl.semaphore_wait(barrier, owners + reps - 2)
-        for k in FAR[:2]:
-            owner_copy(p, k).start()
-
-        @pl.when(inner == 0)
-        def _():
-            for k in FAR[2:]:
-                owner_copy(p, k).start()
-
-        for k in NEAR:
-            owner_copy(p, k).start()
-
-        for group in GROUPS:
-            if group[-1] == p:
-
-                @pl.when(inner == 1)
-                def _():
-                    for late in group:
-                        for k in FAR[2:]:
-                            owner_copy(late, k).start()
+        send_copy(p, far[0])
+        for partner in near:
+            send_copy(p, partner)
+        if p == 0:
+            for partner in far[1:]:
+                send_copy(p, partner)
+        elif p >= LAG:
+            for partner in far[1:]:
+                send_copy(p - LAG + 1, partner)
 
     loads[1].wait()
     send_plane(0, (voxel_ref[...] - 256).astype(f32).astype(bf16))
@@ -306,6 +305,10 @@
     for c in range(COLORS):
         send_plane(3 + c, (wide * color_ref[c].astype(f32)).astype(bf16))
 
+    for p in range(PLANES - LAG + 1, PLANES):
+        for partner in far[1:]:
+            send_copy(p, partner)
+
     mine = pl.ds(pl.multiple_of(me * capacity, capacity), capacity)
     for p in range(PLANES):
         recv1[p, mine] = send1[p, mine]
@@ -315,8 +318,7 @@
         i32, (slots, slots), 1
     )
     before = jnp.where(before, 1.0, 0.0).astype(bf16)
-    for k in FAR + NEAR:
-        owner_meta(k).wait()
+    took(meta_recv1.at[pl.ds(0, owners - 1)], m1_recv)
     lane = lax.broadcasted_iota(i32, (8, LANES), 1)
     even = lax.rem(me, 2) == 0
     pieces = []
@@ -346,21 +348,15 @@
     meta_recv2[my_rep] = meta_send2[my_rep]
 
     def relay(p):
-        for k in FAR + NEAR:
-            owner_copy(p, k).wait_recv()
-        data = recv1[p]
+        took(recv1.at[p, pl.ds(0, (owners - 1) * capacity)], s1_recv.at[p])
+        send2[p] = lax.dot_general(
+            pick2_ref[...], recv1[p], NN, preferred_element_type=f32
+        ).astype(bf16)
         for k in (2, 3, 1):
-            q = quarter_rows(mirrored(my_rep, k))
-            send2[p, q] = lax.dot_general(
-                pick2_ref[q], data, NN, preferred_element_type=f32
-            ).astype(bf16)
             rep_copy(p, k).start()
-        q = quarter_rows(my_rep)
-        final[p, q] = lax.dot_general(pick2_ref[q], data, NN, preferred_element_type=f32).astype(bf16)
+        final[p, quarter_rows(my_rep)] = send2[p, quarter_rows(my_rep)]
 
     def land(p):
-        for k in range(1, reps):
-            rep_copy(p, k).wait_recv()
         data = final[p].astype(f32)
         if p > 0:
             feats_ref[pl.ds(p - 1, slots, stride=8), :] = data
@@ -370,8 +366,7 @@
             feats_ref[pl.ds(6, slots, stride=8), :] = lax.shift_right_logical(voxel, 6).astype(f32)
 
     def list_slots():
-        for k in range(1, reps):
-            rep_meta(k).wait()
+        took(meta_recv2.at[pl.ds(0, reps - 1)], m2_recv)
         lane = lax.broadcasted_iota(i32, (8, LANES), 1)
         row = lax.broadcasted_iota(i32, (8, LANES), 0)
         targets, values = [], []
@@ -408,21 +403,20 @@
         copy.start()
         return copy
 
-    copy = None
     for p in range(PLANES):
         relay(p)
-        if p == 1:
+        if p == 3:
             copy = list_slots()
-        if p >= 2:
-            land(p - 2)
-    land(PLANES - 2)
+    copy.wait()
+    took(final.at[pl.ds(0, PLANES - 1), pl.ds(0, (reps - 1) * quota)], s2_recv.at[0])
+    for p in range(PLANES - 1):
+        land(p)
+    took(final.at[PLANES - 1, pl.ds(0, (reps - 1) * quota)], s2_recv.at[1])
     land(PLANES - 1)
-    copy.wait()
-    for p in range(PLANES):
-        for k in FAR + NEAR:
-            owner_copy(p, k).wait_send()
-        for k in range(1, reps):
-            rep_copy(p, k).wait_send()
+    took(send1.at[:, pl.ds(0, (owners - 1) * capacity)], s1_send)
+    took(send2.at[:, pl.ds(0, (reps - 1) * quota)], s2_send)
+    took(meta_recv1.at[pl.ds(0, owners - 1)], m1_send)
+    took(meta_recv2.at[pl.ds(0, reps - 1)], m2_send)
 
 
 def join_kernel(
@@ -557,14 +551,14 @@
             pltpu.VMEM((reps, 8, LANES), jnp.float32),
             pltpu.VMEM((reps, 8, LANES), jnp.float32),
             pltpu.VMEM(listing, jnp.int32),
-            dma((PLANES, owners)),
-            dma((PLANES, owners)),
-            dma((owners,)),
-            dma((owners,)),
-            dma((PLANES, reps)),
-            dma((PLANES, reps)),
-            dma((reps,)),
-            dma((reps,)),
+            dma,
+            dma((PLANES,)),
+            dma,
+            dma,
+            dma,
+            dma((2,)),
+            dma,
+            dma,
             pltpu.SMEM(send_counts.shape, jnp.int32),
             pltpu.VMEM((1, bins), jnp.int32),
             pltpu.VMEM(table.shape, jnp.int32),

time: 35.1 us -> 33.1 us (0.943)
  Pallas kernels: 34.3 us -> 32.3 us
    pallas_call x1, Pallas kernels: 29.6 us -> 27.6 us  [exchange_call(): pl.pallas_call(lambda *refs: exchange_kernel(owners, reps, OWN // reps, *...]
where the time goes in v2:
time: 33.1 us; the launch traced here: 32.9 us
  Pallas kernels  32.3 us (98%)
  between operations  0.64 us (2%)
    pallas_call x1, Pallas kernels, exchange_call(): pl.pallas_call(lambda *refs: exchange_kernel(owners, reps, OWN // reps, *...  27.6 us
    pallas_call x1, Pallas kernels, join_call(): pl.pallas_call(join_kernel, out_shape=(jax.ShapeDtypeStruct(old_tsdf.shap...  4.67 us

profile of v2, /device:TPU:0, one launch (start us, length us, event | category | flops | bytes accessed | tf_op | source)
XLA Modules:
  0.0 32.9 jit_solution(12540954251746163735)
XLA Ops:
  0.6 27.6 %exchange.1 = (f32[4096,128]{1,0:T(8,128)S(1)}, s32[24,128]{1,0:T(8,128)S(4)}) custom-call(s32[1,8]{1,0:T(1,128)} %refs_0_.1, s32[1,256]{1,0:T(1,128)} %bitcast.5, s32[16,128]{1,0:T(8,128)} %bitcast.4, s32[256,128]{1,0:T(8,128)} %refs_3_.1, bf16[256,128]{1,0:T(8,128)(2,1)} %refs_4_.1, bf16[256,128]{1,0:T(8,128)(2,1)} %refs_5_.1, bf16[3,256,128]{2,1,0:T(8,128)(2,1)} %bitcast.3), custom_call_target="tpu_custom_call" | custom-call | tf_op jit(solution)/shard_map/exchange/pallas_call | solution.py:535
  28.3 4.7 %join.1 = (f32[64,4,512]{2,1,0:T(4,128)}, f32[64,512]{1,0:T(8,128)}) custom-call(s32[24,128]{1,0:T(8,128)S(4)} %get-tuple-element.4.meta_ref, f32[4096,128]{1,0:T(8,128)S(1)} %get-tuple-element.5.feats, f32[64,4,512]{2,1,0:T(4,128)} %tsdf_hbm.1, f32[64,512]{1,0:T(8,128)} %oldw_hbm.1), custom_call_target="tpu_custom_call" | custom-call | tf_op jit(solution)/shard_map/join/pallas_call | solution.py:500
